TPU v7x, 256 devices: a whole 4x4x8 slice. The times are simulated.
256 devices in a mesh: shard: 16 (over z, core), cols: 4 (over y), job: 4 (over x).
Axes of the slice: x: 4, y: 4, z: 8, core: 2. Of those that a mesh axis runs over, the one named last changes fastest.
Arguments:
- one_query: float32 [16384, 4096], P(('job', 'shard'), 'cols'), parts along dimension 0, may hold values from -0.125 to 0.125
- other_query: float32 [16384, 4096], P(('job', 'shard'), 'cols'), parts along dimension 0, may hold values from -0.09375 to 0.09375
- one_key: float32 [16384, 1024], P(('job', 'shard'), 'cols'), parts along dimension 0, may hold values from -0.125 to 0.125
- other_key: float32 [16384, 1024], P(('job', 'shard'), 'cols'), parts along dimension 0, may hold values from -0.09375 to 0.09375
- one_value: float32 [16384, 1024], P(('job', 'shard'), 'cols'), parts along dimension 0, may hold values from -0.125 to 0.125
- other_value: float32 [16384, 1024], P(('job', 'shard'), 'cols'), parts along dimension 0, may hold values from -0.09375 to 0.09375
- mix_share: float32 [16384], P(('job', 'shard')), parts along dimension 0, may hold values from 0.2 to 0.8
- norm_gain: float32 [16384], P(('job', 'shard')), parts along dimension 0, may hold values from 0.25 to 1.75
Outputs:
- final_query: bfloat16 [16384, 4096], P('job', 'cols'), parts along dimension 0
- final_key: bfloat16 [16384, 1024], P('job', 'cols'), parts along dimension 0
- final_value: bfloat16 [16384, 1024], P('job', 'cols'), parts along dimension 0
- scale_query: float32 [16384], P(('job', 'cols')), parts along dimension 0
- scale_key: float32 [4096], P(('job', 'cols')), parts along dimension 0
- scale_value: float32 [4096], P(('job', 'cols')), parts along dimension 0
There are 4 independent parts, one for each index of `job`. A program takes and returns all parts, laid end to end along the dimension named above; each array names one. Nothing has to cross between parts.
All inputs are finite; a program needn't handle non-finite values. Where the computation divides by a largest or mean magnitude, that divisor is 1e-20 or more.
Results may differ from a plain program's by a relative error of at most 0.001.
Values may be sent and summed in bfloat16 or wider, within the bound.
A program may use at most 128 MiB of HBM per device.

v0:
```python
import jax
import jax.numpy as jnp
from jax import lax
from jax.sharding import PartitionSpec as P


def sent_to_all(array, axis):
    copies = jnp.broadcast_to(array, (lax.axis_size(axis), *array.shape))
    return lax.all_to_all(copies, axis, split_axis=0, concat_axis=0, tiled=True)


def taken_together(array, axis):
    everything = sent_to_all(array, axis)
    return jnp.max(everything, axis=0)


def packed_total(arrays, axis):
    flat, at, outs = (jnp.concatenate([a.reshape(-1) for a in arrays]), 0, [])
    total = taken_together(flat, axis)
    for a in arrays:
        outs.append(total[at : at + a.size].reshape(a.shape))
        at += a.size
    return tuple(outs)


def side_by_side(arrays, axis, dim, along):
    widths = [a.shape[along] for a in arrays]
    both = jnp.concatenate(arrays, axis=along)
    whole = lax.all_gather(both, axis, axis=dim, tiled=True)
    return tuple(jnp.split(whole, [sum(widths[:k]) for k in range(1, len(widths))], axis=along))


def shards(
    one_query, other_query, one_key, other_key, one_value, other_value, mix_share, norm_gain
):
    result_query = mix_share[:, None] * one_query + (1.0 - mix_share[:, None]) * other_query
    result_key = mix_share[:, None] * one_key + (1.0 - mix_share[:, None]) * other_key
    result_value = mix_share[:, None] * one_value + (1.0 - mix_share[:, None]) * other_value
    result_gained_query = result_query * norm_gain[:, None]
    result_gained_key = result_key * norm_gain[:, None]
    result_gained_value = result_value * norm_gain[:, None]
    scale_query, scale_key, scale_value = packed_total(
        (
            jnp.max(jnp.abs(result_gained_query), axis=0),
            jnp.max(jnp.abs(result_gained_key), axis=0),
            jnp.max(jnp.abs(result_gained_value), axis=0),
        ),
        "shard",
    )
    narrow_query, narrow_key, narrow_value = (
        (result_gained_query / scale_query).astype(jnp.bfloat16),
        (result_gained_key / scale_key).astype(jnp.bfloat16),
        (result_gained_value / scale_value).astype(jnp.bfloat16),
    )
    final_query, final_key, final_value = side_by_side(
        (narrow_query, narrow_key, narrow_value), "shard", 0, 1
    )
    return (final_query, final_key, final_value, scale_query, scale_key, scale_value)


def solution(mesh):
    placed = (
        P(("job", "shard"), "cols"),
        P(("job", "shard"), "cols"),
        P(("job", "shard"), "cols"),
        P(("job", "shard"), "cols"),
        P(("job", "shard"), "cols"),
        P(("job", "shard"), "cols"),
        P(("job", "shard")),
        P(("job", "shard")),
    )
    return jax.shard_map(
        shards,
        mesh=mesh,
        in_specs=placed,
        out_specs=(
            P("job", "cols"),
            P("job", "cols"),
            P("job", "cols"),
            P(("job", "cols")),
            P(("job", "cols")),
            P(("job", "cols")),
        ),
        check_vma=False,
    )
```

profile of v0, /device:TPU:1, one launch (start us, length us, event | category | flops | bytes accessed | tf_op | source)
XLA Modules:
  0.0 121.3 jit_solution(13329526383472720484)
XLA Ops:
  7.2 0.0 copy-start.5
  7.2 0.0 copy-start.6
  7.2 0.0 copy-start.2
  7.2 0.0 copy-start.3
  7.2 0.0 copy-start
  7.2 0.0 copy-start.1
  7.2 0.0 all-gather.2.cloned.1.call-start
  7.3 0.8 broadcast_subtract_fusion
  8.0 1.8 %abs_reduce_fusion = (f32[1024]{0:T(1024)S(1)}, f32[256,1024]{1,0:T(8,128)S(1)}) fusion(f32[256]{0:T(256)} %param.15, f32[256,1024]{1,0:T(8,128)} %param.9, f32[256]{0:T(256)S(1)} %broadcast_subtract_fusion, f32[256,1024]{1,0:T(8,128)} %param.8, f32[256]{0:T(256)} %param.14), kind=kLoop, calls=%fused_computation.1 | loop fusion | flops 1571840 | bytes 3152896 | tf_op jit(solution)/shard_map/reduce_max | solution.py:44
  9.8 0.0 copy-done.5
  9.9 0.0 copy-done.6
  9.9 0.0 copy-done.2
  9.9 0.0 copy-done.3
  9.9 0.0 copy-done
  9.9 0.0 copy-done.1
  9.9 0.2 abs_reduce_fusion.2
  10.1 0.1 broadcast_in_dim.2
  10.2 18.2 %all_to_all.6 = f32[16,1,1536]{2,1,0:T(1,128)S(1)} all-to-all(f32[16,1,1536]{2,1,0:T(1,128)S(1)} %broadcast_in_dim.2), channel_id=1, replica_groups=mesh['shard'=16,'cols'=4,'job'=4] {'shard'}, dimensions={0} | all-to-all | bytes 196608 | tf_op jit(solution)/shard_map/all_to_all | solution.py:9
  28.4 0.1 reduce_max.39
  28.5 0.0 copy-start.7
  28.5 0.0 copy-start.8
  28.5 0.0 copy-start.4
  28.5 0.1 divide_convert_fusion
  28.7 0.9 pad_maximum_fusion
  29.6 0.0 all-gather.2.cloned.1.call-update
  29.6 0.0 copy-done.7
  29.6 0.0 copy-done.8
  29.7 0.0 copy-done.4
  29.7 72.6 %all-gather.2.cloned.1.call-done = bf16[4096,1536]{1,0:T(8,128)(2,1)} async-done(((bf16[256,1536]{1,0:T(8,128)(2,1)}), bf16[4096,1536]{1,0:T(8,128)(2,1)}) %all-gather.2.cloned.1.call-update) | async-done | bytes 12582928 | tf_op jit(solution)/shard_map/all_gather | solution.py:29
  102.2 4.5 %fusion = (bf16[4096,256]{1,0:T(8,128)(2,1)}, bf16[4096,256]{1,0:T(8,128)(2,1)}) fusion(bf16[4096,1536]{1,0:T(8,128)(2,1)} %all-gather.2.cloned.1.call-done), kind=kLoop, calls=%fused_computation.12 | loop fusion | bytes 8388608 | tf_op jit(solution)/shard_map/split | solution.py:30
  106.7 7.8 %split.12 = bf16[4096,1024]{1,0:T(8,128)(2,1)} slice(bf16[4096,1536]{1,0:T(8,128)(2,1)} %all-gather.2.cloned.1.call-done), slice={[0:4096], [0:1024]} | slice | bytes 16777216 | tf_op jit(solution)/shard_map/split | solution.py:30
  (4 shorter events, 0.1 us)
Async XLA Ops:
  7.2 2.7 %copy-start.5 = (f32[256]{0:T(256)S(1)}, f32[256]{0:T(256)}, u32[]{:S(2)}) copy-start(f32[256]{0:T(256)} %param.14) | copy-start | bytes 3076
  7.2 2.7 %copy-start.6 = (f32[256]{0:T(256)S(1)}, f32[256]{0:T(256)}, u32[]{:S(2)}) copy-start(f32[256]{0:T(256)} %param.15) | copy-start | bytes 3076
  7.2 2.7 %copy-start.2 = (f32[256,256]{1,0:T(8,128)S(1)}, f32[256,256]{1,0:T(8,128)}, u32[]{:S(2)}) copy-start(f32[256,256]{1,0:T(8,128)} %param.13) | copy-start | bytes 786436
  7.2 2.7 %copy-start.3 = (f32[256,256]{1,0:T(8,128)S(1)}, f32[256,256]{1,0:T(8,128)}, u32[]{:S(2)}) copy-start(f32[256,256]{1,0:T(8,128)} %param.12) | copy-start | bytes 786436
  7.2 2.7 %copy-start = (f32[256,256]{1,0:T(8,128)S(1)}, f32[256,256]{1,0:T(8,128)}, u32[]{:S(2)}) copy-start(f32[256,256]{1,0:T(8,128)} %param.11) | copy-start | bytes 786436
  7.2 2.7 %copy-start.1 = (f32[256,256]{1,0:T(8,128)S(1)}, f32[256,256]{1,0:T(8,128)}, u32[]{:S(2)}) copy-start(f32[256,256]{1,0:T(8,128)} %param.10) | copy-start | bytes 786436
  7.2 95.0 %all-gather.2.cloned.1.call-start = ((), (), s32[]{:S(2)}) async-start(), calls=%async_computation.1 | async-start | bytes 13369344 | tf_op jit(solution)/shard_map/all_gather | solution.py:29
  28.5 1.2 copy-start.7
  28.5 1.2 copy-start.8
  28.5 1.1 copy-start.4
Sparse Core Ops, SparseCore 0:
  29.8 72.4 all-gather.1
where the time goes:
time: 122 us; the launch traced here: 121 us
  waiting for transfers between devices  72.6 us (60%)
  blocking collectives  18.2 us (15%)
  between operations  14.2 us (12%)
  local copies, waits for them, and re-layouts  12.4 us (10%)
  other arithmetic  3.9 us (3%)
    all_gather x1, waiting for transfers between devices, side_by_side(): whole = lax.all_gather(both, axis, axis=dim, tiled=True)  72.6 us
    all_to_all x1, blocking collectives, sent_to_all(): return lax.all_to_all(copies, axis, split_axis=0, concat_axis=0, tiled=True)  18.2 us
    split x2, local copies, waits for them, and re-layouts, side_by_side(): jnp.split(whole, [sum(widths[:k]) for k in range(1, len(widths))], axis=a...  12.3 us
  transfers between devices with their start and end apart: 1, of which 1 were waited for; matrix products, arithmetic and copies ran while one was open for 0% of the time, Pallas kernels for 0%

commit v1 on v0

v1 whole, which is shorter than its diff:
```python
import functools

import jax
import jax.numpy as jnp
from jax import lax
from jax.experimental import pallas as pl
from jax.experimental.pallas import tpu as pltpu
from jax.sharding import PartitionSpec as P

MESH = pl.DeviceIdType.MESH
PARTS = 4


def kernel(
    n,
    one_query,
    other_query,
    one_key,
    other_key,
    one_value,
    other_value,
    mix_share,
    norm_gain,
    query,
    key,
    value,
    scale_query,
    scale_key,
    scale_value,
    ins,
    mix_rows,
    gained,
    maxima,
    load_sem,
    max_send,
    max_recv,
    right_send,
    right_recv,
    left_send,
    left_recv,
    side_send,
    side_recv,
):
    one_q, other_q, one_k, other_k, one_v, other_v, share, gain = ins
    mix_a, mix_b = mix_rows
    gained_q, gained_k, gained_v = gained
    rows, wide = one_query.shape
    narrow = one_key.shape[1]
    chips = n // 2
    me = lax.axis_index("shard")
    core = lax.rem(me, 2)
    sibling = me + 1 - 2 * core
    right, left = lax.rem(me + 2, n), lax.rem(me + n - 2, n)

    loads = [
        pltpu.make_async_copy(src, dst, load_sem.at[i])
        for i, (src, dst) in enumerate(
            [
                (mix_share, share),
                (norm_gain, gain),
                (one_key, one_k),
                (other_key, other_k),
                (one_value, one_v),
                (other_value, other_v),
                (one_query, one_q),
                (other_query, other_q),
            ]
        )
    ]
    for load in loads:
        load.start()
    barrier = pltpu.get_barrier_semaphore()
    for d in range(1, n):
        pl.semaphore_signal(
            barrier, inc=1, device_id={"shard": lax.rem(me + d, n)}, device_id_type=MESH
        )

    loads[0].wait()
    loads[1].wait()
    for t in range(rows // 128):
        at = pl.ds(128 * t, 128)
        m = jnp.broadcast_to(share[at].reshape(1, 128), (128, 128)).T
        g = jnp.broadcast_to(gain[at].reshape(1, 128), (128, 128)).T
        mix_a[at, :] = m * g
        mix_b[at, :] = (1.0 - m) * g

    def mixed(one, other, out, first, columns):
        for t in range(columns // 128):
            at = pl.ds(128 * t, 128)
            x = mix_a[...] * one[:, at] + mix_b[...] * other[:, at]
            out[:, at] = x
            maxima[0, :, pl.ds(first + 128 * t, 128)] = jnp.max(
                jnp.abs(x), axis=0, keepdims=True
            )

    loads[2].wait()
    loads[3].wait()
    mixed(one_k, other_k, gained_k, wide, narrow)
    loads[4].wait()
    loads[5].wait()
    mixed(one_v, other_v, gained_v, wide + narrow, narrow)
    loads[6].wait()
    loads[7].wait()
    mixed(one_q, other_q, gained_q, 0, wide)

    pl.semaphore_wait(barrier, n - 1)
    sends = []
    for d in sorted(range(1, n), key=lambda d: -min(d, n - d)):
        copy = pltpu.make_async_remote_copy(
            src_ref=maxima.at[0],
            dst_ref=maxima.at[d],
            send_sem=max_send.at[d],
            recv_sem=max_recv.at[d],
            device_id={"shard": lax.rem(me + d, n)},
            device_id_type=MESH,
        )
        copy.start()
        sends.append(copy)
    for copy in sends:
        copy.wait_recv()
    top = maxima[0]
    for d in range(1, n):
        top = jnp.maximum(top, maxima[d])
    over = 1.0 / top

    chunks = PARTS + 2
    part = rows // PARTS

    def place(owner, k):
        first = owner * rows
        if k < PARTS:
            return query.at[pl.ds(pl.multiple_of(first + k * part, part), part), :]
        out = key if k == PARTS else value
        return out.at[pl.ds(pl.multiple_of(first, rows), rows), :]

    def passed(ref, device, send_sem, recv_sem):
        return pltpu.make_async_remote_copy(
            src_ref=ref,
            dst_ref=ref,
            send_sem=send_sem,
            recv_sem=recv_sem,
            device_id={"shard": device},
            device_id_type=MESH,
        )

    ways = [
        (right, -2, right_send, right_recv, [k for k in range(chunks) if k % 2 == 0]),
        (left, 2, left_send, left_recv, [k for k in range(chunks) if k % 2 == 1]),
    ]
    steps = chips // 2
    started = []

    def onward(way, step, k):
        device, back, send_sem, recv_sem, last = ways[way]
        if step < steps - 1 or (step == steps - 1 and k in last):
            ref = place(lax.rem(me + back * step + 2 * n, n), k)
            copy = passed(ref, device, send_sem.at[step, k], recv_sem.at[step, k])
            copy.start()
            started.append(copy)

    def aside(slot, owner, k):
        copy = passed(place(owner, k), sibling, side_send.at[slot, k], side_recv.at[slot, k])
        copy.start()
        started.append(copy)
        beside.append((slot, owner, k))

    beside = []
    for k in range(chunks):
        if k < PARTS:
            x = gained_q[pl.ds(k * part, part), :] * over[:, :wide]
        elif k == PARTS:
            x = gained_k[...] * over[:, wide : wide + narrow]
        else:
            x = gained_v[...] * over[:, wide + narrow :]
        place(me, k)[...] = x.astype(jnp.bfloat16)
        onward(0, 0, k)
        onward(1, 0, k)
        aside(0, me, k)
    scale_query[...] = top[0, :wide]
    scale_key[...] = top[0, wide : wide + narrow]
    scale_value[...] = top[0, wide + narrow :]

    for step in range(steps):
        for k in range(chunks):
            for way, (device, back, send_sem, recv_sem, last) in enumerate(ways):
                if step == steps - 1 and k not in last:
                    continue
                owner = lax.rem(me + back * (step + 1) + 2 * n, n)
                passed(
                    place(owner, k), device, send_sem.at[step, k], recv_sem.at[step, k]
                ).wait_recv()
                onward(way, step + 1, k)
                slot = 1 + 2 * step + (way if step < steps - 1 else 0)
                aside(slot, owner, k)

    for slot, owner, k in beside:
        theirs = owner + 1 - 2 * core
        passed(
            place(theirs, k), sibling, side_send.at[slot, k], side_recv.at[slot, k]
        ).wait_recv()
    for copy in sends + started:
        copy.wait_send()


def stored(*refs):
    count = len(refs) // 2
    sems = refs[-1]
    copies = [
        pltpu.make_async_copy(src, dst, sems.at[i])
        for i, (src, dst) in enumerate(zip(refs[:count], refs[count:-1]))
    ]
    for copy in copies:
        copy.start()
    for copy in copies:
        copy.wait()


def shards(
    one_query, other_query, one_key, other_key, one_value, other_value, mix_share, norm_gain
):
    n = lax.axis_size("shard")
    rows, wide = one_query.shape
    narrow = one_key.shape[1]
    chunks, steps = PARTS + 2, n // 4
    full = (rows, wide), (rows, wide), (rows, narrow), (rows, narrow), (rows, narrow), (rows, narrow)
    hbm = pl.BlockSpec(memory_space=pltpu.HBM)
    vmem = pl.BlockSpec(memory_space=pltpu.VMEM)
    outs = [
        pltpu.VMEM(shape, dtype)
        for shape, dtype in [
            ((n * rows, wide), jnp.bfloat16),
            ((n * rows, narrow), jnp.bfloat16),
            ((n * rows, narrow), jnp.bfloat16),
            ((wide,), jnp.float32),
            ((narrow,), jnp.float32),
            ((narrow,), jnp.float32),
        ]
    ]
    whole = pl.pallas_call(
        functools.partial(kernel, n),
        out_shape=outs,
        in_specs=[hbm] * 8,
        out_specs=[vmem] * 6,
        scratch_shapes=[
            tuple(pltpu.VMEM(shape, jnp.float32) for shape in full)
            + (pltpu.VMEM((rows,), jnp.float32),) * 2,
            (pltpu.VMEM((rows, 128), jnp.float32),) * 2,
            tuple(pltpu.VMEM(shape, jnp.float32) for shape in full[::2]),
            pltpu.VMEM((n, 1, wide + 2 * narrow), jnp.float32),
            pltpu.SemaphoreType.DMA((8,)),
            pltpu.SemaphoreType.DMA((n,)),
            pltpu.SemaphoreType.DMA((n,)),
            pltpu.SemaphoreType.DMA((steps, chunks)),
            pltpu.SemaphoreType.DMA((steps, chunks)),
            pltpu.SemaphoreType.DMA((steps, chunks)),
            pltpu.SemaphoreType.DMA((steps, chunks)),
            pltpu.SemaphoreType.DMA((n // 2, chunks)),
            pltpu.SemaphoreType.DMA((n // 2, chunks)),
        ],
        compiler_params=pltpu.CompilerParams(
            collective_id=0, has_side_effects=True, vmem_limit_bytes=24 * 2**20
        ),
    )(
        *(
            pltpu.with_memory_space_constraint(x, pltpu.HBM)
            for x in (
                one_query,
                other_query,
                one_key,
                other_key,
                one_value,
                other_value,
                mix_share,
                norm_gain,
            )
        )
    )
    return pl.pallas_call(
        stored,
        out_shape=[pltpu.HBM(x.shape, x.dtype) for x in whole],
        in_specs=[vmem] * 6,
        out_specs=[hbm] * 6,
        scratch_shapes=[pltpu.SemaphoreType.DMA((6,))],
        compiler_params=pltpu.CompilerParams(vmem_limit_bytes=2**20),
    )(*whole)


def solution(mesh):
    placed = (
        P(("job", "shard"), "cols"),
        P(("job", "shard"), "cols"),
        P(("job", "shard"), "cols"),
        P(("job", "shard"), "cols"),
        P(("job", "shard"), "cols"),
        P(("job", "shard"), "cols"),
        P(("job", "shard")),
        P(("job", "shard")),
    )
    return jax.shard_map(
        shards,
        mesh=mesh,
        in_specs=placed,
        out_specs=(
            P("job", "cols"),
            P("job", "cols"),
            P("job", "cols"),
            P(("job", "cols")),
            P(("job", "cols")),
            P(("job", "cols")),
        ),
        check_vma=False,
    )
```

time: 122 us -> 84.1 us (0.69)
  Pallas kernels: 0 us -> 83.3 us
  waiting for transfers between devices: 72.6 us -> 0 us
  blocking collectives: 18.2 us -> 0 us
  between operations: 14.2 us -> 0.64 us
  local copies, waits for them, and re-layouts: 12.4 us -> 0 us
  other arithmetic: 3.9 us -> 0 us
    pallas_call x0 -> x2, Pallas kernels: none -> 83.3 us  [the longest x1 78.6 us: shards(): pl.pallas_call(functools.partial(kernel, n), out_shape=outs, in_specs=[hb...]
    all_gather x1 -> x0, waiting for transfers between devices: 72.6 us -> none  [side_by_side(): whole = lax.all_gather(both, axis, axis=dim, tiled=True)]
    all_to_all x1 -> x0, blocking collectives: 18.2 us -> none  [sent_to_all(): return lax.all_to_all(copies, axis, split_axis=0, concat_axis=0, tiled=True)]
    split x2 -> x0, local copies, waits for them, and re-layouts: 12.3 us -> none  [side_by_side(): jnp.split(whole, [sum(widths[:k]) for k in range(1, len(widths))], axis=a...]
    reduce_max x3 -> x0, other arithmetic: 2.06 us -> none  [the longest x1 1.8 us: shards(): jnp.max(jnp.abs(result_gained_query), axis=0)]
  transfers between devices with their start and end apart: 1 -> 0, of which waited for: 1 -> 0; matrix products, arithmetic and copies ran while one was open for 0% -> 0% of each run, Pallas kernels for 0% -> 0%
where the time goes in v1:
time: 84.1 us; the launch traced here: 84 us
  Pallas kernels  83.3 us (99%)
    pallas_call x1, Pallas kernels, shards(): pl.pallas_call(functools.partial(kernel, n), out_shape=outs, in_specs=[hb...  78.6 us
    pallas_call x1, Pallas kernels, shards(): pl.pallas_call(stored, out_shape=[pltpu.HBM(x.shape, x.dtype) for x in wh...  4.77 us

profile of v1, /device:TPU:1, one launch (start us, length us, event | category | flops | bytes accessed | tf_op | source)
XLA Modules:
  0.0 84.0 jit_solution(11540721679210148999)
XLA Ops:
  0.6 78.6 %shard_map.127 = (bf16[4096,1024]{1,0:T(8,128)(2,1)S(1)}, bf16[4096,256]{1,0:T(8,128)(2,1)S(1)}, bf16[4096,256]{1,0:T(8,128)(2,1)S(1)}, f32[1024]{0:T(1024)S(1)}, f32[256]{0:T(256)S(1)}, /*index=5*/f32[256]{0:T(256)S(1)}) custom-call(f32[256,1024]{1,0:T(8,128)} %one_query.1, f32[256,1024]{1,0:T(8,128)} %other_query.1, f32[256,256]{1,0:T(8,128)} %one_key.1, ...), custom_call_target="tpu_custom_call" | custom-call | tf_op jit(solution)/shard_map/pallas_call | solution.py:239
  79.2 4.8 %shard_map.128 = (bf16[4096,1024]{1,0:T(8,128)(2,1)}, bf16[4096,256]{1,0:T(8,128)(2,1)}, bf16[4096,256]{1,0:T(8,128)(2,1)}, f32[1024]{0:T(1024)}, f32[256]{0:T(256)}, /*index=5*/f32[256]{0:T(256)}) custom-call(bf16[4096,1024]{1,0:T(8,128)(2,1)S(1)} %get-tuple-element.12.refs_0_, bf16[4096,256]{1,0:T(8,128)(2,1)S(1)} %get-tuple-element.13.refs_1_, ...), custom_call_target="tpu_custom_call" | custom-call | tf_op jit(solution)/shard_map/pallas_call | solution.py:278

commit v2 on v1

v2 whole, which is shorter than its diff:
```python
import functools

import jax
import jax.numpy as jnp
from jax import lax
from jax.experimental import pallas as pl
from jax.experimental.pallas import tpu as pltpu
from jax.sharding import PartitionSpec as P

MESH = pl.DeviceIdType.MESH
STORES = 2


def kernel(
    n,
    pieces,
    one_query,
    other_query,
    one_key,
    other_key,
    one_value,
    other_value,
    mix_share,
    norm_gain,
    whole,
    scale_query,
    scale_key,
    scale_value,
    ins,
    mix_a,
    mix_b,
    gained,
    maxima,
    load_sem,
    max_sem,
    send_sem,
    side_sem,
    right_recv,
    left_recv,
):
    one_q, other_q, one_k, other_k, one_v, other_v, share, gain = ins
    rows, wide = one_query.shape
    narrow = one_key.shape[1]
    chips = n // 2
    me = lax.axis_index("shard")
    core = lax.rem(me, 2)
    sibling = me + 1 - 2 * core
    right, left = lax.rem(me + 2, n), lax.rem(me + n - 2, n)

    barrier = pltpu.get_barrier_semaphore()
    for d in range(1, n):
        pl.semaphore_signal(
            barrier, inc=1, device_id={"shard": lax.rem(me + d, n)}, device_id_type=MESH
        )
    loads = [
        pltpu.make_async_copy(src, dst, load_sem.at[i])
        for i, (src, dst) in enumerate(
            [
                (mix_share, share),
                (norm_gain, gain),
                (one_key, one_k),
                (other_key, other_k),
                (one_value, one_v),
                (other_value, other_v),
                (one_query, one_q),
                (other_query, other_q),
            ]
        )
    ]
    for load in loads:
        load.start()

    loads[0].wait()
    loads[1].wait()
    for t in range(rows // 128):
        at = pl.ds(128 * t, 128)
        m = jnp.broadcast_to(share[at].reshape(1, 128), (128, 128)).T
        g = jnp.broadcast_to(gain[at].reshape(1, 128), (128, 128)).T
        mix_a[at, :] = m * g
        mix_b[at, :] = (1.0 - m) * g

    def mixed(one, other, first, columns):
        for t in range(columns // 128):
            at, to = pl.ds(128 * t, 128), pl.ds(first + 128 * t, 128)
            x = mix_a[...] * one[:, at] + mix_b[...] * other[:, at]
            gained[:, to] = x
            maxima[0, :, to] = jnp.max(jnp.abs(x), axis=0, keepdims=True)

    loads[2].wait()
    loads[3].wait()
    mixed(one_k, other_k, wide, narrow)
    loads[4].wait()
    loads[5].wait()
    mixed(one_v, other_v, wide + narrow, narrow)
    loads[6].wait()
    loads[7].wait()
    mixed(one_q, other_q, 0, wide)

    def sent(src, dst, device, send, recv):
        return pltpu.make_async_remote_copy(
            src_ref=src,
            dst_ref=dst,
            send_sem=send,
            recv_sem=recv,
            device_id={"shard": device},
            device_id_type=MESH,
        )

    pl.semaphore_wait(barrier, n - 1)
    for d in sorted(range(1, n), key=lambda d: -min(d, n - d)):
        sent(maxima.at[0], maxima.at[d], lax.rem(me + d, n), max_sem.at[0], max_sem.at[1]).start()
    others = maxima.at[pl.ds(1, n - 1)]
    all_maxima = sent(others, others, right, max_sem.at[0], max_sem.at[1])
    all_maxima.wait_recv()
    top = maxima[0]
    for d in range(1, n):
        top = jnp.maximum(top, maxima[d])
    over = 1.0 / top

    def place(owner, k):
        first, count = pieces[k]
        return whole.at[pl.ds(pl.multiple_of(owner * rows + first, 8), count), :]

    steps, count = chips // 2, len(pieces)
    ways = [
        (right, -2, right_recv, range(count // 2)),
        (left, 2, left_recv, range(count // 2, count)),
    ]

    def onward(way, step, k):
        device, back, recv, last = ways[way]
        if step < steps - 1 or (step == steps - 1 and k in last):
            ref = place(lax.rem(me + back * step + 2 * n, n), k)
            sent(ref, ref, device, send_sem.at[0], recv.at[step, k]).start()

    def aside(owner, k):
        ref = place(owner, k)
        sent(ref, ref, sibling, send_sem.at[0], side_sem.at[0]).start()

    for k, (first, many) in enumerate(pieces):
        x = gained[pl.ds(first, many), :] * over
        place(me, k)[...] = x.astype(jnp.bfloat16)
        onward(0, 0, k)
        onward(1, 0, k)
        aside(me, k)
    scale_query[...] = top[0, :wide]
    scale_key[...] = top[0, wide : wide + narrow]
    scale_value[...] = top[0, wide + narrow :]

    for step in range(steps):
        for k in range(count):
            for way, (device, back, recv, last) in enumerate(ways):
                if step == steps - 1 and k not in last:
                    continue
                owner = lax.rem(me + back * (step + 1) + 2 * n, n)
                ref = place(owner, k)
                sent(ref, ref, device, send_sem.at[0], recv.at[step, k]).wait_recv()
                onward(way, step + 1, k)
                aside(owner, k)

    theirs = whole.at[pl.ds(0, chips * rows), :]
    sent(theirs, theirs, sibling, send_sem.at[0], side_sem.at[0]).wait_recv()
    onwards = whole.at[pl.ds(0, (2 * chips - 1) * rows), :]
    sent(onwards, onwards, sibling, send_sem.at[0], side_sem.at[0]).wait_send()
    all_maxima.wait_send()


def stored(whole, one, two, three, query, key, value, scale_query, scale_key, scale_value, sems):
    length = whole.shape[0] // STORES
    at, copies = 0, []
    for out in (query, key, value):
        for p in range(STORES):
            part = pl.ds(p * length, length)
            copies.append((whole.at[part, pl.ds(at, out.shape[1])], out.at[part, :]))
        at += out.shape[1]
    copies += [(one, scale_query), (two, scale_key), (three, scale_value)]
    copies = [
        pltpu.make_async_copy(src, dst, sems.at[i]) for i, (src, dst) in enumerate(copies)
    ]
    for copy in copies:
        copy.start()
    for copy in copies:
        copy.wait()


def shards(
    one_query, other_query, one_key, other_key, one_value, other_value, mix_share, norm_gain
):
    n = lax.axis_size("shard")
    rows, wide = one_query.shape
    narrow = one_key.shape[1]
    width = wide + 2 * narrow
    quarter = rows // 4
    pieces = [(k * quarter, quarter) for k in range(4)]
    steps = n // 4
    full = [(rows, wide)] * 2 + [(rows, narrow)] * 4
    hbm = pl.BlockSpec(memory_space=pltpu.HBM)
    vmem = pl.BlockSpec(memory_space=pltpu.VMEM)
    scales = [((wide,), jnp.float32), ((narrow,), jnp.float32), ((narrow,), jnp.float32)]
    gathered = pl.pallas_call(
        functools.partial(kernel, n, pieces),
        out_shape=[pltpu.VMEM((n * rows, width), jnp.bfloat16)]
        + [pltpu.VMEM(shape, dtype) for shape, dtype in scales],
        in_specs=[hbm] * 8,
        out_specs=[vmem] * 4,
        scratch_shapes=[
            tuple(pltpu.VMEM(shape, jnp.float32) for shape in full)
            + (pltpu.VMEM((rows,), jnp.float32),) * 2,
            pltpu.VMEM((rows, 128), jnp.float32),
            pltpu.VMEM((rows, 128), jnp.float32),
            pltpu.VMEM((rows, width), jnp.float32),
            pltpu.VMEM((n, 1, width), jnp.float32),
            pltpu.SemaphoreType.DMA((8,)),
            pltpu.SemaphoreType.DMA((2,)),
            pltpu.SemaphoreType.DMA((1,)),
            pltpu.SemaphoreType.DMA((1,)),
            pltpu.SemaphoreType.DMA((steps, len(pieces))),
            pltpu.SemaphoreType.DMA((steps, len(pieces))),
        ],
        compiler_params=pltpu.CompilerParams(
            collective_id=0, has_side_effects=True, vmem_limit_bytes=24 * 2**20
        ),
    )(
        *(
            pltpu.with_memory_space_constraint(x, pltpu.HBM)
            for x in (
                one_query,
                other_query,
                one_key,
                other_key,
                one_value,
                other_value,
                mix_share,
                norm_gain,
            )
        )
    )
    outs = [((n * rows, wide), jnp.bfloat16)] + [((n * rows, narrow), jnp.bfloat16)] * 2 + scales
    return pl.pallas_call(
        stored,
        out_shape=[pltpu.HBM(shape, dtype) for shape, dtype in outs],
        in_specs=[vmem] * 4,
        out_specs=[hbm] * 6,
        scratch_shapes=[pltpu.SemaphoreType.DMA((3 * STORES + 3,))],
        compiler_params=pltpu.CompilerParams(vmem_limit_bytes=2**20),
    )(*gathered)


def solution(mesh):
    placed = (
        P(("job", "shard"), "cols"),
        P(("job", "shard"), "cols"),
        P(("job", "shard"), "cols"),
        P(("job", "shard"), "cols"),
        P(("job", "shard"), "cols"),
        P(("job", "shard"), "cols"),
        P(("job", "shard")),
        P(("job", "shard")),
    )
    return jax.shard_map(
        shards,
        mesh=mesh,
        in_specs=placed,
        out_specs=(
            P("job", "cols"),
            P("job", "cols"),
            P("job", "cols"),
            P(("job", "cols")),
            P(("job", "cols")),
            P(("job", "cols")),
        ),
        check_vma=False,
    )
```

time: 84.1 us -> 82.6 us (0.982)
  Pallas kernels: 83.3 us -> 81.8 us
    pallas_call x2, Pallas kernels: 83.3 us -> 81.8 us  [the longest x1 77.2 us: shards(): pl.pallas_call(functools.partial(kernel, n, pieces), out_shape=[pltpu.VME...]
where the time goes in v2:
time: 82.6 us; the launch traced here: 82.5 us
  Pallas kernels  81.8 us (99%)
    pallas_call x1, Pallas kernels, shards(): pl.pallas_call(functools.partial(kernel, n, pieces), out_shape=[pltpu.VME...  77.2 us
    pallas_call x1, Pallas kernels, shards(): pl.pallas_call(stored, out_shape=[pltpu.HBM(shape, dtype) for shape, dtyp...  4.65 us

profile of v2, /device:TPU:1, one launch (start us, length us, event | category | flops | bytes accessed | tf_op | source)
XLA Modules:
  0.0 82.5 jit_solution(14974724030263669383)
XLA Ops:
  0.6 77.2 %shard_map.127 = (bf16[4096,1536]{1,0:T(8,128)(2,1)S(1)}, f32[1024]{0:T(1024)S(1)}, f32[256]{0:T(256)S(1)}, f32[256]{0:T(256)S(1)}) custom-call(f32[256,1024]{1,0:T(8,128)} %one_query.1, f32[256,1024]{1,0:T(8,128)} %other_query.1, f32[256,256]{1,0:T(8,128)} %one_key.1, f32[256,256]{1,0:T(8,128)} %other_key.1, f32[256,256]{1,0:T(8,128)} %one_value.1, ...), custom_call_target="tpu_custom_call" | custom-call | tf_op jit(solution)/shard_map/pallas_call | solution.py:200
  77.8 4.6 %shard_map.128 = (bf16[4096,1024]{1,0:T(8,128)(2,1)}, bf16[4096,256]{1,0:T(8,128)(2,1)}, bf16[4096,256]{1,0:T(8,128)(2,1)}, f32[1024]{0:T(1024)}, f32[256]{0:T(256)}, /*index=5*/f32[256]{0:T(256)}) custom-call(bf16[4096,1536]{1,0:T(8,128)(2,1)S(1)} %get-tuple-element.10.whole, f32[1024]{0:T(1024)S(1)} %get-tuple-element.11.one, ...), custom_call_target="tpu_custom_call" | custom-call | tf_op jit(solution)/shard_map/pallas_call | solution.py:239

commit v3 on v2

--- a/solution.py
+++ b/solution.py
@@ -9,6 +9,7 @@
 
 MESH = pl.DeviceIdType.MESH
 STORES = 2
+AHEAD = 64
 
 
 def kernel(
@@ -31,8 +32,11 @@
     mix_b,
     gained,
     maxima,
+    early,
+    ahead,
     load_sem,
     max_sem,
+    ahead_sem,
     send_sem,
     side_sem,
     right_recv,
@@ -41,17 +45,33 @@
     one_q, other_q, one_k, other_k, one_v, other_v, share, gain = ins
     rows, wide = one_query.shape
     narrow = one_key.shape[1]
-    chips = n // 2
+    chips, tiles = n // 2, (wide + 2 * narrow) // 128
     me = lax.axis_index("shard")
     core = lax.rem(me, 2)
     sibling = me + 1 - 2 * core
     right, left = lax.rem(me + 2, n), lax.rem(me + n - 2, n)
 
+    chip = me // 2
+    first, second = chip == 0, chip == 1
     barrier = pltpu.get_barrier_semaphore()
     for d in range(1, n):
-        pl.semaphore_signal(
-            barrier, inc=1, device_id={"shard": lax.rem(me + d, n)}, device_id_type=MESH
-        )
+        peer = lax.rem(me + d, n)
+
+        @pl.when((peer // 2 != 1) | (chip <= 1))
+        def _():
+            pl.semaphore_signal(barrier, inc=1, device_id={"shard": peer}, device_id_type=MESH)
+
+    blank = jnp.zeros(maxima.shape[1:], jnp.float32)
+
+    @pl.when(second)
+    def _():
+        maxima[lax.rem(me - sibling + n, n)] = blank
+
+    @pl.when(jnp.logical_not(second))
+    def _():
+        maxima[lax.rem(me - 2 + n, n)] = blank
+        maxima[lax.rem(me - 3 + n, n)] = blank
+
     loads = [
         pltpu.make_async_copy(src, dst, load_sem.at[i])
         for i, (src, dst) in enumerate(
@@ -84,7 +104,7 @@
             at, to = pl.ds(128 * t, 128), pl.ds(first + 128 * t, 128)
             x = mix_a[...] * one[:, at] + mix_b[...] * other[:, at]
             gained[:, to] = x
-            maxima[0, :, to] = jnp.max(jnp.abs(x), axis=0, keepdims=True)
+            maxima[0, pl.ds(first // 128 + t, 1), :] = jnp.max(jnp.abs(x), axis=0, keepdims=True)
 
     loads[2].wait()
     loads[3].wait()
@@ -106,63 +126,141 @@
             device_id_type=MESH,
         )
 
-    pl.semaphore_wait(barrier, n - 1)
-    for d in sorted(range(1, n), key=lambda d: -min(d, n - d)):
-        sent(maxima.at[0], maxima.at[d], lax.rem(me + d, n), max_sem.at[0], max_sem.at[1]).start()
-    others = maxima.at[pl.ds(1, n - 1)]
-    all_maxima = sent(others, others, right, max_sem.at[0], max_sem.at[1])
-    all_maxima.wait_recv()
+    early_maxima = sent(maxima.at[0], early, left, max_sem.at[0], ahead_sem.at[0])
+    early_rows = sent(gained.at[pl.ds(0, AHEAD), :], ahead, left, ahead_sem.at[1], ahead_sem.at[2])
+
+    @pl.when(second)
+    def _():
+        pl.semaphore_wait(barrier, 3)
+        early_maxima.start()
+        early_rows.start()
+
+    @pl.when(jnp.logical_not(second))
+    def _():
+        @pl.when(first)
+        def _():
+            early_maxima.wait_recv()
+            maxima[0] = jnp.maximum(maxima[0], early[...])
+
+        pl.semaphore_wait(barrier, n - 1)
+        for d in sorted(range(1, n), key=lambda d: -min(d, n - d)):
+            peer = lax.rem(me + d, n)
+            sent(maxima.at[0], maxima.at[d], peer, max_sem.at[0], max_sem.at[1]).start()
+
+    def heard(count):
+        some = maxima.at[pl.ds(0, count)]
+        return sent(some, some, right, max_sem.at[0], max_sem.at[1])
+
+    @pl.when(second)
+    def _():
+        heard(n - 2).wait_recv()
+
+    @pl.when(jnp.logical_not(second))
+    def _():
+        heard(n - 3).wait_recv()
+
     top = maxima[0]
     for d in range(1, n):
         top = jnp.maximum(top, maxima[d])
     over = 1.0 / top
 
     def place(owner, k):
-        first, count = pieces[k]
-        return whole.at[pl.ds(pl.multiple_of(owner * rows + first, 8), count), :]
+        start, many = pieces[k]
+        return whole.at[pl.ds(pl.multiple_of(owner * rows + start, 8), many), :]
 
     steps, count = chips // 2, len(pieces)
-    ways = [
-        (right, -2, right_recv, range(count // 2)),
-        (left, 2, left_recv, range(count // 2, count)),
-    ]
+    ways = [(right, -2, right_recv, (0, 2, 4)), (left, 2, left_recv, (1, 3))]
+    moved, early_piece = 2, 4
+
+    def when(condition, run):
+        if condition is True:
+            run()
+        elif condition is not False:
+            pl.when(condition)(run)
+
+    def goes(way, step, k, into_first):
+        if step == steps - 1 and k == moved:
+            return into_first if way == 1 else jnp.logical_not(into_first)
+        if step == steps - 1:
+            return k in ways[way][3]
+        return step < steps
 
     def onward(way, step, k):
         device, back, recv, last = ways[way]
-        if step < steps - 1 or (step == steps - 1 and k in last):
+
+        def run():
             ref = place(lax.rem(me + back * step + 2 * n, n), k)
             sent(ref, ref, device, send_sem.at[0], recv.at[step, k]).start()
+
+        condition = goes(way, step, k, second if way == 1 else chip == chips - 1)
+        if way == 1 and step == 0 and k == early_piece:
+            condition = jnp.logical_not(second)
+        when(condition, run)
 
     def aside(owner, k):
         ref = place(owner, k)
         sent(ref, ref, sibling, send_sem.at[0], side_sem.at[0]).start()
 
-    for k, (first, many) in enumerate(pieces):
-        x = gained[pl.ds(first, many), :] * over
-        place(me, k)[...] = x.astype(jnp.bfloat16)
+    def scaled(rows_of, to):
+        for t in range(tiles):
+            at = pl.ds(128 * t, 128)
+            to[:, at] = (rows_of[:, at] * over[t : t + 1, :]).astype(jnp.bfloat16)
+
+    for k, (start, many) in enumerate(pieces):
+        scaled(gained.at[pl.ds(start, many), :], place(me, k))
         onward(0, 0, k)
         onward(1, 0, k)
         aside(me, k)
-    scale_query[...] = top[0, :wide]
-    scale_key[...] = top[0, wide : wide + narrow]
-    scale_value[...] = top[0, wide + narrow :]
+    t = 0
+    for out in (scale_query, scale_key, scale_value):
+        for p in range(out.shape[0] // 128):
+            out[pl.ds(128 * p, 128)] = top[t, :]
+            t += 1
 
     for step in range(steps):
         for k in range(count):
             for way, (device, back, recv, last) in enumerate(ways):
-                if step == steps - 1 and k not in last:
-                    continue
                 owner = lax.rem(me + back * (step + 1) + 2 * n, n)
                 ref = place(owner, k)
-                sent(ref, ref, device, send_sem.at[0], recv.at[step, k]).wait_recv()
-                onward(way, step + 1, k)
-                aside(owner, k)
+                arrived = sent(ref, ref, device, send_sem.at[0], recv.at[step, k])
+                if way == 1 and step == 0 and k == early_piece:
+
+                    @pl.when(first)
+                    def _():
+                        early_rows.wait_recv()
+                        scaled(ahead, ref)
+
+                    pl.when(jnp.logical_not(first))(arrived.wait_recv)
+                    onward(way, step + 1, k)
+                    aside(owner, k)
+                    continue
+
+                def run():
+                    arrived.wait_recv()
+                    onward(way, step + 1, k)
+                    aside(owner, k)
+
+                when(goes(way, step, k, first), run)
 
     theirs = whole.at[pl.ds(0, chips * rows), :]
     sent(theirs, theirs, sibling, send_sem.at[0], side_sem.at[0]).wait_recv()
-    onwards = whole.at[pl.ds(0, (2 * chips - 1) * rows), :]
-    sent(onwards, onwards, sibling, send_sem.at[0], side_sem.at[0]).wait_send()
-    all_maxima.wait_send()
+    def all_sent(count):
+        onwards = whole.at[pl.ds(0, count), :]
+        sent(onwards, onwards, sibling, send_sem.at[0], side_sem.at[0]).wait_send()
+
+    everything, less = (2 * chips - 1) * rows, pieces[moved][1]
+
+    @pl.when(second)
+    def _():
+        all_sent(everything + less - AHEAD)
+        early_maxima.wait_send()
+        early_rows.wait_send()
+
+    @pl.when(jnp.logical_not(second))
+    def _():
+        heard(n - 1).wait_send()
+        pl.when(chip == chips - 1)(lambda: all_sent(everything - less))
+        pl.when(chip != chips - 1)(lambda: all_sent(everything))
 
 
 def stored(whole, one, two, three, query, key, value, scale_query, scale_key, scale_value, sems):
@@ -175,11 +273,13 @@
         at += out.shape[1]
     copies += [(one, scale_query), (two, scale_key), (three, scale_value)]
     copies = [
-        pltpu.make_async_copy(src, dst, sems.at[i]) for i, (src, dst) in enumerate(copies)
+        pltpu.make_async_copy(src, dst, sems.at[max(0, i - 3 * STORES + 1)])
+        for i, (src, dst) in enumerate(copies)
     ]
     for copy in copies:
         copy.start()
-    for copy in copies:
+    pltpu.make_async_copy(whole, whole, sems.at[0]).wait()
+    for copy in copies[3 * STORES :]:
         copy.wait()
 
 
@@ -190,8 +290,15 @@
     rows, wide = one_query.shape
     narrow = one_key.shape[1]
     width = wide + 2 * narrow
-    quarter = rows // 4
-    pieces = [(k * quarter, quarter) for k in range(4)]
+    half, small = rows // 2, 16
+    turn = half - AHEAD // 2
+    pieces = [
+        (AHEAD, turn - AHEAD),
+        (half, half - small),
+        (turn, half - turn),
+        (rows - small, small),
+        (0, AHEAD),
+    ]
     steps = n // 4
     full = [(rows, wide)] * 2 + [(rows, narrow)] * 4
     hbm = pl.BlockSpec(memory_space=pltpu.HBM)
@@ -209,9 +316,12 @@
             pltpu.VMEM((rows, 128), jnp.float32),
             pltpu.VMEM((rows, 128), jnp.float32),
             pltpu.VMEM((rows, width), jnp.float32),
-            pltpu.VMEM((n, 1, width), jnp.float32),
+            pltpu.VMEM((n, width // 128, 128), jnp.float32),
+            pltpu.VMEM((width // 128, 128), jnp.float32),
+            pltpu.VMEM((AHEAD, width), jnp.float32),
             pltpu.SemaphoreType.DMA((8,)),
             pltpu.SemaphoreType.DMA((2,)),
+            pltpu.SemaphoreType.DMA((3,)),
             pltpu.SemaphoreType.DMA((1,)),
             pltpu.SemaphoreType.DMA((1,)),
             pltpu.SemaphoreType.DMA((steps, len(pieces))),
@@ -241,7 +351,7 @@
         out_shape=[pltpu.HBM(shape, dtype) for shape, dtype in outs],
         in_specs=[vmem] * 4,
         out_specs=[hbm] * 6,
-        scratch_shapes=[pltpu.SemaphoreType.DMA((3 * STORES + 3,))],
+        scratch_shapes=[pltpu.SemaphoreType.DMA((4,))],
         compiler_params=pltpu.CompilerParams(vmem_limit_bytes=2**20),
     )(*gathered)
 

time: 82.6 us -> 80.1 us (0.970)
  Pallas kernels: 81.8 us -> 79.3 us
    pallas_call x1, Pallas kernels: 77.2 us -> 74.7 us  [shards(): pl.pallas_call(functools.partial(kernel, n, pieces), out_shape=[pltpu.VME...]
where the time goes in v3:
time: 80.1 us; the launch traced here: 80 us
  Pallas kernels  79.3 us (99%)
    pallas_call x1, Pallas kernels, shards(): pl.pallas_call(functools.partial(kernel, n, pieces), out_shape=[pltpu.VME...  74.7 us
    pallas_call x1, Pallas kernels, shards(): pl.pallas_call(stored, out_shape=[pltpu.HBM(shape, dtype) for shape, dtyp...  4.6 us

profile of v3, /device:TPU:1, one launch (start us, length us, event | category | flops | bytes accessed | tf_op | source)
XLA Modules:
  0.0 80.0 jit_solution(8986143497343523769)
XLA Ops:
  0.6 74.7 %shard_map.127 = (bf16[4096,1536]{1,0:T(8,128)(2,1)S(1)}, f32[1024]{0:T(1024)S(1)}, f32[256]{0:T(256)S(1)}, f32[256]{0:T(256)S(1)}) custom-call(f32[256,1024]{1,0:T(8,128)} %one_query.1, f32[256,1024]{1,0:T(8,128)} %other_query.1, f32[256,256]{1,0:T(8,128)} %one_key.1, f32[256,256]{1,0:T(8,128)} %other_key.1, f32[256,256]{1,0:T(8,128)} %one_value.1, ...), custom_call_target="tpu_custom_call" | custom-call | tf_op jit(solution)/shard_map/pallas_call | solution.py:307
  75.4 4.6 %shard_map.128 = (bf16[4096,1024]{1,0:T(8,128)(2,1)}, bf16[4096,256]{1,0:T(8,128)(2,1)}, bf16[4096,256]{1,0:T(8,128)(2,1)}, f32[1024]{0:T(1024)}, f32[256]{0:T(256)}, /*index=5*/f32[256]{0:T(256)}) custom-call(bf16[4096,1536]{1,0:T(8,128)(2,1)S(1)} %get-tuple-element.10.whole, f32[1024]{0:T(1024)S(1)} %get-tuple-element.11.one, ...), custom_call_target="tpu_custom_call" | custom-call | tf_op jit(solution)/shard_map/pallas_call | solution.py:349

commit v4 on v3

--- a/solution.py
+++ b/solution.py
@@ -9,12 +9,13 @@
 
 MESH = pl.DeviceIdType.MESH
 STORES = 2
-AHEAD = 64
+AHEAD = 48
 
 
 def kernel(
     n,
     pieces,
+    turned,
     one_query,
     other_query,
     one_key,
@@ -32,11 +33,14 @@
     mix_b,
     gained,
     maxima,
-    early,
+    far,
+    merged,
+    whole_top,
     ahead,
     load_sem,
     max_sem,
     ahead_sem,
+    near_sem,
     send_sem,
     side_sem,
     right_recv,
@@ -51,26 +55,22 @@
     sibling = me + 1 - 2 * core
     right, left = lax.rem(me + 2, n), lax.rem(me + n - 2, n)
 
-    chip = me // 2
-    first, second = chip == 0, chip == 1
+    chip, half = me // 2, n // 2
+    early = chip < chips // 2
+    late = jnp.logical_not(early)
+    base = half * (me // half)
     barrier = pltpu.get_barrier_semaphore()
-    for d in range(1, n):
-        peer = lax.rem(me + d, n)
-
-        @pl.when((peer // 2 != 1) | (chip <= 1))
-        def _():
-            pl.semaphore_signal(barrier, inc=1, device_id={"shard": peer}, device_id_type=MESH)
-
-    blank = jnp.zeros(maxima.shape[1:], jnp.float32)
-
-    @pl.when(second)
-    def _():
-        maxima[lax.rem(me - sibling + n, n)] = blank
-
-    @pl.when(jnp.logical_not(second))
-    def _():
-        maxima[lax.rem(me - 2 + n, n)] = blank
-        maxima[lax.rem(me - 3 + n, n)] = blank
+
+    def greet(device):
+        pl.semaphore_signal(barrier, inc=1, device_id={"shard": device}, device_id_type=MESH)
+
+    for d in range(1, half):
+        greet(base + lax.rem(me + d, half))
+
+    @pl.when(early)
+    def _():
+        for d in range(half):
+            greet(half + d)
 
     loads = [
         pltpu.make_async_copy(src, dst, load_sem.at[i])
@@ -126,42 +126,82 @@
             device_id_type=MESH,
         )
 
-    early_maxima = sent(maxima.at[0], early, left, max_sem.at[0], ahead_sem.at[0])
-    early_rows = sent(gained.at[pl.ds(0, AHEAD), :], ahead, left, ahead_sem.at[1], ahead_sem.at[2])
-
-    @pl.when(second)
-    def _():
-        pl.semaphore_wait(barrier, 3)
-        early_maxima.start()
-        early_rows.start()
-
-    @pl.when(jnp.logical_not(second))
-    def _():
-        @pl.when(first)
+    lower, upper = chip == 0, chip == chips // 2 - 1
+    to_right, to_left = chip < chips // 2 - 1, early & (chip > 0)
+    from_left, from_right = to_left, to_right
+    mine = maxima.at[0]
+
+    def within(d):
+        sent(
+            mine, maxima.at[d], base + lax.rem(me + d, half), max_sem.at[0], max_sem.at[1]
+        ).start()
+
+    def heard(ref, count, recv):
+        some = ref.at[pl.ds(0, count)]
+        return sent(some, some, right, max_sem.at[0], recv)
+
+    def merged_to(device):
+        return sent(merged, merged, device, max_sem.at[4], max_sem.at[3])
+
+    early_rows = gained.at[pl.ds(0, AHEAD), :]
+    right_rows = sent(early_rows, ahead.at[0], right, ahead_sem.at[0], ahead_sem.at[2])
+    left_rows = sent(early_rows, ahead.at[1], left, ahead_sem.at[1], ahead_sem.at[3])
+
+    @pl.when(early)
+    def _():
+        pl.semaphore_wait(barrier, half - 1)
+        for d in range(1, half):
+            within(d)
+        pl.when(to_right)(right_rows.start)
+        pl.when(to_left)(left_rows.start)
+
+    @pl.when(late)
+    def _():
+        pl.semaphore_wait(barrier, n - 1)
+        close = core + (half - 2) * (1 - chip // (chips * 3 // 4))
+        pl.semaphore_signal(near_sem, inc=1, device_id={"shard": close}, device_id_type=MESH)
+        for d in sorted(range(half), key=lambda d: -min(d + 1, half - d)):
+            peer = lax.rem(me + half // 2 + 1 + d, half)
+            sent(mine, far.at[me - half], peer, max_sem.at[0], max_sem.at[2]).start()
+        for d in range(1, half):
+            within(d)
+
+    heard(maxima, half - 1, max_sem.at[1]).wait_recv()
+    top = maxima[0]
+    for d in range(1, half):
+        top = jnp.maximum(top, maxima[d])
+
+    @pl.when(lower | upper)
+    def _():
+        merged[...] = top
+        pl.semaphore_wait(near_sem, 2)
+
+        @pl.when(lower)
         def _():
-            early_maxima.wait_recv()
-            maxima[0] = jnp.maximum(maxima[0], early[...])
-
-        pl.semaphore_wait(barrier, n - 1)
-        for d in sorted(range(1, n), key=lambda d: -min(d, n - d)):
-            peer = lax.rem(me + d, n)
-            sent(maxima.at[0], maxima.at[d], peer, max_sem.at[0], max_sem.at[1]).start()
-
-    def heard(count):
-        some = maxima.at[pl.ds(0, count)]
-        return sent(some, some, right, max_sem.at[0], max_sem.at[1])
-
-    @pl.when(second)
-    def _():
-        heard(n - 2).wait_recv()
-
-    @pl.when(jnp.logical_not(second))
-    def _():
-        heard(n - 3).wait_recv()
-
-    top = maxima[0]
-    for d in range(1, n):
-        top = jnp.maximum(top, maxima[d])
+            merged_to(n - 2 + core).start()
+            merged_to(n - 4 + core).start()
+
+        @pl.when(upper)
+        def _():
+            merged_to(half + core).start()
+            merged_to(half + 2 + core).start()
+
+    whole_top[...] = top
+
+    @pl.when(early)
+    def _():
+        heard(far, half, max_sem.at[2]).wait_recv()
+        most = whole_top[...]
+        for d in range(half):
+            most = jnp.maximum(most, far[d])
+        whole_top[...] = most
+
+    @pl.when(late)
+    def _():
+        merged_to(right).wait_recv()
+        whole_top[...] = jnp.maximum(whole_top[...], merged[...])
+
+    top = whole_top[...]
     over = 1.0 / top
 
     def place(owner, k):
@@ -169,8 +209,7 @@
         return whole.at[pl.ds(pl.multiple_of(owner * rows + start, 8), many), :]
 
     steps, count = chips // 2, len(pieces)
-    ways = [(right, -2, right_recv, (0, 2, 4)), (left, 2, left_recv, (1, 3))]
-    moved, early_piece = 2, 4
+    ways = [(right, -2, right_recv), (left, 2, left_recv)]
 
     def when(condition, run):
         if condition is True:
@@ -178,23 +217,32 @@
         elif condition is not False:
             pl.when(condition)(run)
 
-    def goes(way, step, k, into_first):
-        if step == steps - 1 and k == moved:
-            return into_first if way == 1 else jnp.logical_not(into_first)
-        if step == steps - 1:
-            return k in ways[way][3]
-        return step < steps
+    def any_of(chosen):
+        condition = False
+        for c in chosen:
+            condition = (chip == c) | condition
+        return condition if chosen else False
+
+    def goes(way, step, k, shift):
+        if step < steps - 1:
+            return True
+        if step == steps:
+            return False
+        to = 1 if way == 0 else -1
+        takers = [c for c in range(chips) if (k in turned[c]) == (way == 0)]
+        senders = [(c - shift * to) % chips for c in takers]
+        return True if len(senders) == chips else any_of(senders)
 
     def onward(way, step, k):
-        device, back, recv, last = ways[way]
+        device, back, recv = ways[way]
 
         def run():
             ref = place(lax.rem(me + back * step + 2 * n, n), k)
             sent(ref, ref, device, send_sem.at[0], recv.at[step, k]).start()
 
-        condition = goes(way, step, k, second if way == 1 else chip == chips - 1)
-        if way == 1 and step == 0 and k == early_piece:
-            condition = jnp.logical_not(second)
+        condition = goes(way, step, k, 1)
+        if step == 0 and k == 0:
+            condition = jnp.logical_not(to_left if way == 1 else to_right)
         when(condition, run)
 
     def aside(owner, k):
@@ -219,18 +267,19 @@
 
     for step in range(steps):
         for k in range(count):
-            for way, (device, back, recv, last) in enumerate(ways):
+            for way, (device, back, recv) in enumerate(ways):
                 owner = lax.rem(me + back * (step + 1) + 2 * n, n)
                 ref = place(owner, k)
                 arrived = sent(ref, ref, device, send_sem.at[0], recv.at[step, k])
-                if way == 1 and step == 0 and k == early_piece:
-
-                    @pl.when(first)
+                if step == 0 and k == 0:
+                    came = from_left if way == 0 else from_right
+
+                    @pl.when(came)
                     def _():
-                        early_rows.wait_recv()
-                        scaled(ahead, ref)
-
-                    pl.when(jnp.logical_not(first))(arrived.wait_recv)
+                        (right_rows if way == 0 else left_rows).wait_recv()
+                        scaled(ahead.at[way], ref)
+
+                    pl.when(jnp.logical_not(came))(arrived.wait_recv)
                     onward(way, step + 1, k)
                     aside(owner, k)
                     continue
@@ -240,27 +289,38 @@
                     onward(way, step + 1, k)
                     aside(owner, k)
 
-                when(goes(way, step, k, first), run)
+                when(goes(way, step, k, 0), run)
 
     theirs = whole.at[pl.ds(0, chips * rows), :]
     sent(theirs, theirs, sibling, send_sem.at[0], side_sem.at[0]).wait_recv()
-    def all_sent(count):
-        onwards = whole.at[pl.ds(0, count), :]
-        sent(onwards, onwards, sibling, send_sem.at[0], side_sem.at[0]).wait_send()
-
-    everything, less = (2 * chips - 1) * rows, pieces[moved][1]
-
-    @pl.when(second)
-    def _():
-        all_sent(everything + less - AHEAD)
-        early_maxima.wait_send()
-        early_rows.wait_send()
-
-    @pl.when(jnp.logical_not(second))
-    def _():
-        heard(n - 1).wait_send()
-        pl.when(chip == chips - 1)(lambda: all_sent(everything - less))
-        pl.when(chip != chips - 1)(lambda: all_sent(everything))
+    by_right = [sum(pieces[k][1] for k in turned[c]) for c in range(chips)]
+    totals = {}
+    for c in range(chips):
+        total = (2 * chips - 1) * rows + by_right[(c + 1) % chips] - by_right[c - 1]
+        total -= AHEAD * ((c < chips // 2 - 1) + (0 < c < chips // 2))
+        totals.setdefault(total, []).append(c)
+    for total, chosen in totals.items():
+
+        @pl.when(any_of(chosen))
+        def _():
+            onwards = whole.at[pl.ds(0, total), :]
+            sent(onwards, onwards, sibling, send_sem.at[0], side_sem.at[0]).wait_send()
+
+    @pl.when(early)
+    def _():
+        heard(maxima, half - 1, max_sem.at[1]).wait_send()
+        pl.when(to_right)(right_rows.wait_send)
+        pl.when(to_left)(left_rows.wait_send)
+
+    @pl.when(late)
+    def _():
+        both = maxima.at[pl.ds(0, n - 1)]
+        sent(both, both, right, max_sem.at[0], max_sem.at[1]).wait_send()
+
+    @pl.when(lower | upper)
+    def _():
+        both = maxima.at[pl.ds(0, 2)]
+        sent(both, both, right, max_sem.at[4], max_sem.at[3]).wait_send()
 
 
 def stored(whole, one, two, three, query, key, value, scale_query, scale_key, scale_value, sems):
@@ -290,22 +350,29 @@
     rows, wide = one_query.shape
     narrow = one_key.shape[1]
     width = wide + 2 * narrow
-    half, small = rows // 2, 16
-    turn = half - AHEAD // 2
+    middle, small = rows // 2, 16
+    moved = AHEAD // 2
     pieces = [
-        (AHEAD, turn - AHEAD),
-        (half, half - small),
-        (turn, half - turn),
+        (0, AHEAD),
+        (middle + moved, middle - moved - small),
+        (AHEAD, middle - moved - AHEAD),
+        (middle, moved),
+        (middle - moved, moved),
         (rows - small, small),
-        (0, AHEAD),
     ]
+    chips = n // 2
+    turned = [(0, 2, 4)] * chips
+    turned[0] = (0, 2)
+    turned[chips // 2 - 1] = (0, 2, 3, 4)
+    turned[chips // 2] = (0, 2)
+    turned[chips - 1] = (0, 2, 3, 4)
     steps = n // 4
     full = [(rows, wide)] * 2 + [(rows, narrow)] * 4
     hbm = pl.BlockSpec(memory_space=pltpu.HBM)
     vmem = pl.BlockSpec(memory_space=pltpu.VMEM)
     scales = [((wide,), jnp.float32), ((narrow,), jnp.float32), ((narrow,), jnp.float32)]
     gathered = pl.pallas_call(
-        functools.partial(kernel, n, pieces),
+        functools.partial(kernel, n, pieces, turned),
         out_shape=[pltpu.VMEM((n * rows, width), jnp.bfloat16)]
         + [pltpu.VMEM(shape, dtype) for shape, dtype in scales],
         in_specs=[hbm] * 8,
@@ -317,11 +384,14 @@
             pltpu.VMEM((rows, 128), jnp.float32),
             pltpu.VMEM((rows, width), jnp.float32),
             pltpu.VMEM((n, width // 128, 128), jnp.float32),
+            pltpu.VMEM((n // 2, width // 128, 128), jnp.float32),
             pltpu.VMEM((width // 128, 128), jnp.float32),
-            pltpu.VMEM((AHEAD, width), jnp.float32),
+            pltpu.VMEM((width // 128, 128), jnp.float32),
+            pltpu.VMEM((2, AHEAD, width), jnp.float32),
             pltpu.SemaphoreType.DMA((8,)),
-            pltpu.SemaphoreType.DMA((2,)),
-            pltpu.SemaphoreType.DMA((3,)),
+            pltpu.SemaphoreType.DMA((5,)),
+            pltpu.SemaphoreType.DMA((4,)),
+            pltpu.SemaphoreType.REGULAR,
             pltpu.SemaphoreType.DMA((1,)),
             pltpu.SemaphoreType.DMA((1,)),
             pltpu.SemaphoreType.DMA((steps, len(pieces))),

time: 80.1 us -> 79.6 us (level)
  no operation moved by 1% of the time
where the time goes in v4:
time: 79.6 us; the launch traced here: 79.5 us
  Pallas kernels  78.9 us (99%)
    pallas_call x1, Pallas kernels, shards(): pl.pallas_call(functools.partial(kernel, n, pieces, turned), out_shape=[p...  74.3 us
    pallas_call x1, Pallas kernels, shards(): pl.pallas_call(stored, out_shape=[pltpu.HBM(shape, dtype) for shape, dtyp...  4.6 us

profile of v4, /device:TPU:1, one launch (start us, length us, event | category | flops | bytes accessed | tf_op | source)
XLA Modules:
  0.0 79.5 jit_solution(17983211402183141164)
XLA Ops:
  0.6 74.3 %shard_map.127 = (bf16[4096,1536]{1,0:T(8,128)(2,1)S(1)}, f32[1024]{0:T(1024)S(1)}, f32[256]{0:T(256)S(1)}, f32[256]{0:T(256)S(1)}) custom-call(f32[256,1024]{1,0:T(8,128)} %one_query.1, f32[256,1024]{1,0:T(8,128)} %other_query.1, f32[256,256]{1,0:T(8,128)} %one_key.1, f32[256,256]{1,0:T(8,128)} %other_key.1, f32[256,256]{1,0:T(8,128)} %one_value.1, ...), custom_call_target="tpu_custom_call" | custom-call | tf_op jit(solution)/shard_map/pallas_call | solution.py:374
  74.9 4.6 %shard_map.128 = (bf16[4096,1024]{1,0:T(8,128)(2,1)}, bf16[4096,256]{1,0:T(8,128)(2,1)}, bf16[4096,256]{1,0:T(8,128)(2,1)}, f32[1024]{0:T(1024)}, f32[256]{0:T(256)}, /*index=5*/f32[256]{0:T(256)}) custom-call(bf16[4096,1536]{1,0:T(8,128)(2,1)S(1)} %get-tuple-element.10.whole, f32[1024]{0:T(1024)S(1)} %get-tuple-element.11.one, ...), custom_call_target="tpu_custom_call" | custom-call | tf_op jit(solution)/shard_map/pallas_call | solution.py:419

commit v5 on v4

--- a/solution.py
+++ b/solution.py
@@ -223,6 +223,10 @@
             condition = (chip == c) | condition
         return condition if chosen else False
 
+    crossed = (6, 3)
+    givers = (chips - 1, 1)
+    odd, even = core == 1, core == 0
+
     def goes(way, step, k, shift):
         if step < steps - 1:
             return True
@@ -233,20 +237,55 @@
         senders = [(c - shift * to) % chips for c in takers]
         return True if len(senders) == chips else any_of(senders)
 
+    groups = [(0,), (3, 1, 5), (2, 6, 4)]
+    comes = [[k for k in range(count) if any((k in t) == (way == 0) for t in turned)] for way in range(2)]
+
+    def of_group(owner, g):
+        start = pieces[groups[g][0]][0]
+        many = sum(pieces[k][1] for k in groups[g])
+        return whole.at[pl.ds(pl.multiple_of(owner * rows + start, 8), many), :]
+
+    def group_onward(way, step, g):
+        device, back, recv = ways[way]
+
+        def run():
+            ref = of_group(lax.rem(me + back * step + 2 * n, n), g)
+            sent(ref, ref, device, send_sem.at[0], recv.at[step * len(groups) + g]).start()
+
+        ahead_too = step == 0 and g == 0
+        when(jnp.logical_not(to_left if way == 1 else to_right) if ahead_too else True, run)
+
+    def last_sem(way, k):
+        return ways[way][2].at[(steps - 1) * len(groups) + comes[way].index(k)]
+
     def onward(way, step, k):
         device, back, recv = ways[way]
+        if k not in comes[way]:
+            return
 
         def run():
             ref = place(lax.rem(me + back * step + 2 * n, n), k)
-            sent(ref, ref, device, send_sem.at[0], recv.at[step, k]).start()
+            sent(ref, ref, device, send_sem.at[0], last_sem(way, k)).start()
 
         condition = goes(way, step, k, 1)
-        if step == 0 and k == 0:
-            condition = jnp.logical_not(to_left if way == 1 else to_right)
+        if step == steps - 1 and k == crossed[way]:
+            condition = condition & jnp.logical_not((chip == givers[way]) & even)
         when(condition, run)
 
-    def aside(owner, k):
+    def aside(owner, k, sem=0):
         ref = place(owner, k)
+        sent(ref, ref, sibling, send_sem.at[0], side_sem.at[sem]).start()
+
+    def handed(way):
+        owner = lax.rem(2 * chip + (-2, 2)[way] * (steps - 1) + 2 * n, n)
+        return owner, place(owner, crossed[way])
+
+    def taken(way):
+        owner = lax.rem(2 * chip + (-2, 2)[way] * steps + 2 * n, n)
+        return owner, place(owner, crossed[way])
+
+    def group_aside(owner, g):
+        ref = of_group(owner, g)
         sent(ref, ref, sibling, send_sem.at[0], side_sem.at[0]).start()
 
     def scaled(rows_of, to):
@@ -254,24 +293,27 @@
             at = pl.ds(128 * t, 128)
             to[:, at] = (rows_of[:, at] * over[t : t + 1, :]).astype(jnp.bfloat16)
 
-    for k, (start, many) in enumerate(pieces):
-        scaled(gained.at[pl.ds(start, many), :], place(me, k))
-        onward(0, 0, k)
-        onward(1, 0, k)
-        aside(me, k)
+    for g, group in enumerate(groups):
+        for k in group:
+            start, many = pieces[k]
+            scaled(gained.at[pl.ds(start, many), :], place(me, k))
+        group_onward(0, 0, g)
+        group_onward(1, 0, g)
+        group_aside(me, g)
     t = 0
     for out in (scale_query, scale_key, scale_value):
         for p in range(out.shape[0] // 128):
             out[pl.ds(128 * p, 128)] = top[t, :]
             t += 1
 
-    for step in range(steps):
-        for k in range(count):
+    for step in range(steps - 1):
+        for g, group in enumerate(groups):
             for way, (device, back, recv) in enumerate(ways):
                 owner = lax.rem(me + back * (step + 1) + 2 * n, n)
-                ref = place(owner, k)
-                arrived = sent(ref, ref, device, send_sem.at[0], recv.at[step, k])
-                if step == 0 and k == 0:
+                ref = of_group(owner, g)
+                sem = recv.at[step * len(groups) + g]
+                arrived = sent(ref, ref, device, send_sem.at[0], sem)
+                if step == 0 and g == 0:
                     came = from_left if way == 0 else from_right
 
                     @pl.when(came)
@@ -280,31 +322,93 @@
                         scaled(ahead.at[way], ref)
 
                     pl.when(jnp.logical_not(came))(arrived.wait_recv)
+                else:
+                    arrived.wait_recv()
+                if step < steps - 2:
+                    group_onward(way, step + 1, g)
+                    group_aside(owner, g)
+                    continue
+                for k in group:
                     onward(way, step + 1, k)
+                if crossed[way] not in group:
+                    group_aside(owner, g)
+                    continue
+                hands = (chip == givers[way]) & even
+
+                @pl.when(hands)
+                def _():
+                    for k in group:
+                        aside(owner, k, int(k == crossed[way]))
+
+                pl.when(jnp.logical_not(hands))(lambda: group_aside(owner, g))
+
+                @pl.when((chip == givers[way]) & odd)
+                def _():
+                    _, ref = handed(way)
+                    sent(ref, ref, sibling, send_sem.at[0], side_sem.at[1]).wait_recv()
+                    sent(ref, ref, device, send_sem.at[0], side_sem.at[2 + way]).start()
+
+    for k in (k for group in groups for k in group):
+        for way, (device, back, recv) in enumerate(ways):
+            if k not in comes[way]:
+                continue
+            owner = lax.rem(me + back * steps + 2 * n, n)
+            ref = place(owner, k)
+            arrived = sent(ref, ref, device, send_sem.at[0], last_sem(way, k))
+
+            def run():
+                arrived.wait_recv()
+                aside(owner, k)
+
+            condition = goes(way, steps - 1, k, 0)
+            if k == crossed[way]:
+                condition = condition & jnp.logical_not(lower & even)
+            when(condition, run)
+            if k == crossed[way]:
+
+                @pl.when(lower & odd)
+                def _():
+                    owner, ref = taken(way)
+                    sent(ref, ref, device, send_sem.at[0], side_sem.at[2 + way]).wait_recv()
                     aside(owner, k)
-                    continue
-
-                def run():
-                    arrived.wait_recv()
-                    onward(way, step + 1, k)
-                    aside(owner, k)
-
-                when(goes(way, step, k, 0), run)
-
-    theirs = whole.at[pl.ds(0, chips * rows), :]
-    sent(theirs, theirs, sibling, send_sem.at[0], side_sem.at[0]).wait_recv()
+
+    more = [pieces[k][1] for k in crossed]
+    got, gave = {}, {}
+
     by_right = [sum(pieces[k][1] for k in turned[c]) for c in range(chips)]
-    totals = {}
     for c in range(chips):
         total = (2 * chips - 1) * rows + by_right[(c + 1) % chips] - by_right[c - 1]
         total -= AHEAD * ((c < chips // 2 - 1) + (0 < c < chips // 2))
-        totals.setdefault(total, []).append(c)
-    for total, chosen in totals.items():
-
-        @pl.when(any_of(chosen))
-        def _():
-            onwards = whole.at[pl.ds(0, total), :]
-            sent(onwards, onwards, sibling, send_sem.at[0], side_sem.at[0]).wait_send()
+        for j in range(2):
+            sign, shift = 2 * j - 1, 0
+            if c == 0:
+                shift = sum(more)
+            if c in givers:
+                shift += more[givers.index(c)]
+            gave.setdefault(total + sign * shift, []).append((c, j))
+            count = chips * rows
+            if c == 0:
+                count -= sign * sum(more)
+            if c in givers and j == 1:
+                count -= more[givers.index(c)]
+            got.setdefault(count, []).append((c, j))
+
+    def one_of(chosen):
+        whole_chips = [c for c, j in chosen if j == 0 and (c, 1) in chosen]
+        condition = any_of(whole_chips)
+        for c, j in chosen:
+            if c not in whole_chips:
+                condition = ((chip == c) & (core == j)) | condition
+        return condition
+
+    for kind, totals in (("got", got), ("gave", gave)):
+        for total, chosen in totals.items():
+
+            @pl.when(one_of(chosen))
+            def _():
+                ref = whole.at[pl.ds(0, total), :]
+                copy = sent(ref, ref, sibling, send_sem.at[0], side_sem.at[0])
+                copy.wait_recv() if kind == "got" else copy.wait_send()
 
     @pl.when(early)
     def _():
@@ -355,17 +459,18 @@
     pieces = [
         (0, AHEAD),
         (middle + moved, middle - moved - small),
-        (AHEAD, middle - moved - AHEAD),
+        (AHEAD, middle - 2 * moved - AHEAD),
         (middle, moved),
         (middle - moved, moved),
         (rows - small, small),
+        (middle - 2 * moved, moved),
     ]
     chips = n // 2
-    turned = [(0, 2, 4)] * chips
-    turned[0] = (0, 2)
-    turned[chips // 2 - 1] = (0, 2, 3, 4)
-    turned[chips // 2] = (0, 2)
-    turned[chips - 1] = (0, 2, 3, 4)
+    turned = [(0, 2, 4, 6)] * chips
+    turned[0] = (0, 2, 6)
+    turned[chips // 2 - 1] = (0, 2, 3, 4, 6)
+    turned[chips // 2] = (0, 2, 6)
+    turned[chips - 1] = (0, 2, 3, 4, 6)
     steps = n // 4
     full = [(rows, wide)] * 2 + [(rows, narrow)] * 4
     hbm = pl.BlockSpec(memory_space=pltpu.HBM)
@@ -393,9 +498,9 @@
             pltpu.SemaphoreType.DMA((4,)),
             pltpu.SemaphoreType.REGULAR,
             pltpu.SemaphoreType.DMA((1,)),
-            pltpu.SemaphoreType.DMA((1,)),
-            pltpu.SemaphoreType.DMA((steps, len(pieces))),
-            pltpu.SemaphoreType.DMA((steps, len(pieces))),
+            pltpu.SemaphoreType.DMA((4,)),
+            pltpu.SemaphoreType.DMA((3 * steps + 2,)),
+            pltpu.SemaphoreType.DMA((3 * steps + 1,)),
         ],
         compiler_params=pltpu.CompilerParams(
             collective_id=0, has_side_effects=True, vmem_limit_bytes=24 * 2**20

time: 79.6 us -> 79.1 us (level)
  no operation moved by 1% of the time
where the time goes in v5:
time: 79.1 us; the launch traced here: 79 us
  Pallas kernels  78.3 us (99%)
    pallas_call x1, Pallas kernels, shards(): pl.pallas_call(functools.partial(kernel, n, pieces, turned), out_shape=[p...  73.7 us
    pallas_call x1, Pallas kernels, shards(): pl.pallas_call(stored, out_shape=[pltpu.HBM(shape, dtype) for shape, dtyp...  4.6 us

profile of v5, /device:TPU:1, one launch (start us, length us, event | category | flops | bytes accessed | tf_op | source)
XLA Modules:
  0.0 79.0 jit_solution(9469826746821514690)
XLA Ops:
  0.6 73.7 %shard_map.127 = (bf16[4096,1536]{1,0:T(8,128)(2,1)S(1)}, f32[1024]{0:T(1024)S(1)}, f32[256]{0:T(256)S(1)}, f32[256]{0:T(256)S(1)}) custom-call(f32[256,1024]{1,0:T(8,128)} %one_query.1, f32[256,1024]{1,0:T(8,128)} %other_query.1, f32[256,256]{1,0:T(8,128)} %one_key.1, f32[256,256]{1,0:T(8,128)} %other_key.1, f32[256,256]{1,0:T(8,128)} %one_value.1, ...), custom_call_target="tpu_custom_call" | custom-call | tf_op jit(solution)/shard_map/pallas_call | solution.py:479
  74.4 4.6 %shard_map.128 = (bf16[4096,1024]{1,0:T(8,128)(2,1)}, bf16[4096,256]{1,0:T(8,128)(2,1)}, bf16[4096,256]{1,0:T(8,128)(2,1)}, f32[1024]{0:T(1024)}, f32[256]{0:T(256)}, /*index=5*/f32[256]{0:T(256)}) custom-call(bf16[4096,1536]{1,0:T(8,128)(2,1)S(1)} %get-tuple-element.10.whole, f32[1024]{0:T(1024)S(1)} %get-tuple-element.11.one, ...), custom_call_target="tpu_custom_call" | custom-call | tf_op jit(solution)/shard_map/pallas_call | solution.py:524

commit v6 on v5

--- a/solution.py
+++ b/solution.py
@@ -455,7 +455,7 @@
     narrow = one_key.shape[1]
     width = wide + 2 * narrow
     middle, small = rows // 2, 16
-    moved = AHEAD // 2
+    moved = 32
     pieces = [
         (0, AHEAD),
         (middle + moved, middle - moved - small),

time: 79.1 us -> 79 us (level)
  no operation moved by 1% of the time
where the time goes in v6:
time: 79 us; the launch traced here: 78.9 us
  Pallas kernels  78.2 us (99%)
    pallas_call x1, Pallas kernels, shards(): pl.pallas_call(functools.partial(kernel, n, pieces, turned), out_shape=[p...  73.6 us
    pallas_call x1, Pallas kernels, shards(): pl.pallas_call(stored, out_shape=[pltpu.HBM(shape, dtype) for shape, dtyp...  4.6 us

profile of v6, /device:TPU:1, one launch (start us, length us, event | category | flops | bytes accessed | tf_op | source)
XLA Modules:
  0.0 78.9 jit_solution(17857217818921931793)
XLA Ops:
  0.6 73.6 %shard_map.127 = (bf16[4096,1536]{1,0:T(8,128)(2,1)S(1)}, f32[1024]{0:T(1024)S(1)}, f32[256]{0:T(256)S(1)}, f32[256]{0:T(256)S(1)}) custom-call(f32[256,1024]{1,0:T(8,128)} %one_query.1, f32[256,1024]{1,0:T(8,128)} %other_query.1, f32[256,256]{1,0:T(8,128)} %one_key.1, f32[256,256]{1,0:T(8,128)} %other_key.1, f32[256,256]{1,0:T(8,128)} %one_value.1, ...), custom_call_target="tpu_custom_call" | custom-call | tf_op jit(solution)/shard_map/pallas_call | solution.py:479
  74.3 4.6 %shard_map.128 = (bf16[4096,1024]{1,0:T(8,128)(2,1)}, bf16[4096,256]{1,0:T(8,128)(2,1)}, bf16[4096,256]{1,0:T(8,128)(2,1)}, f32[1024]{0:T(1024)}, f32[256]{0:T(256)}, /*index=5*/f32[256]{0:T(256)}) custom-call(bf16[4096,1536]{1,0:T(8,128)(2,1)S(1)} %get-tuple-element.10.whole, f32[1024]{0:T(1024)S(1)} %get-tuple-element.11.one, ...), custom_call_target="tpu_custom_call" | custom-call | tf_op jit(solution)/shard_map/pallas_call | solution.py:524

commit v7 on v6

--- a/solution.py
+++ b/solution.py
@@ -9,7 +9,7 @@
 
 MESH = pl.DeviceIdType.MESH
 STORES = 2
-AHEAD = 48
+AHEAD = 40
 
 
 def kernel(
@@ -455,7 +455,7 @@
     narrow = one_key.shape[1]
     width = wide + 2 * narrow
     middle, small = rows // 2, 16
-    moved = 32
+    moved = 40
     pieces = [
         (0, AHEAD),
         (middle + moved, middle - moved - small),

time: 79 us -> 79.8 us (1.010)
  Pallas kernels: 78.2 us -> 79 us
    pallas_call x1, Pallas kernels: 73.6 us -> 74.4 us  [shards(): pl.pallas_call(functools.partial(kernel, n, pieces, turned), out_shape=[p...]
where the time goes in v7:
time: 79.8 us; the launch traced here: 79.7 us
  Pallas kernels  79 us (99%)
    pallas_call x1, Pallas kernels, shards(): pl.pallas_call(functools.partial(kernel, n, pieces, turned), out_shape=[p...  74.4 us
    pallas_call x1, Pallas kernels, shards(): pl.pallas_call(stored, out_shape=[pltpu.HBM(shape, dtype) for shape, dtyp...  4.6 us

profile of v7, /device:TPU:1, one launch (start us, length us, event | category | flops | bytes accessed | tf_op | source)
XLA Modules:
  0.0 79.7 jit_solution(13894018169117698944)
XLA Ops:
  0.6 74.4 %shard_map.127 = (bf16[4096,1536]{1,0:T(8,128)(2,1)S(1)}, f32[1024]{0:T(1024)S(1)}, f32[256]{0:T(256)S(1)}, f32[256]{0:T(256)S(1)}) custom-call(f32[256,1024]{1,0:T(8,128)} %one_query.1, f32[256,1024]{1,0:T(8,128)} %other_query.1, f32[256,256]{1,0:T(8,128)} %one_key.1, f32[256,256]{1,0:T(8,128)} %other_key.1, f32[256,256]{1,0:T(8,128)} %one_value.1, ...), custom_call_target="tpu_custom_call" | custom-call | tf_op jit(solution)/shard_map/pallas_call | solution.py:479
  75.1 4.6 %shard_map.128 = (bf16[4096,1024]{1,0:T(8,128)(2,1)}, bf16[4096,256]{1,0:T(8,128)(2,1)}, bf16[4096,256]{1,0:T(8,128)(2,1)}, f32[1024]{0:T(1024)}, f32[256]{0:T(256)}, /*index=5*/f32[256]{0:T(256)}) custom-call(bf16[4096,1536]{1,0:T(8,128)(2,1)S(1)} %get-tuple-element.10.whole, f32[1024]{0:T(1024)S(1)} %get-tuple-element.11.one, ...), custom_call_target="tpu_custom_call" | custom-call | tf_op jit(solution)/shard_map/pallas_call | solution.py:524
